TPU v7x, 128 devices: a whole 4x4x4 slice. The times are simulated.
128 devices in a mesh: row: 16 (over y_hi, z, core), col: 8 (over y_lo, x).
Axes of the slice: x: 4, y: 4 (y_hi: 2, y_lo: 2; y = y_hi * 2 + y_lo), z: 4, core: 2. Of those that a mesh axis runs over, the one named last changes fastest.
Arguments:
- pair: bfloat16 [1024, 1024, 128], P('row', 'col'), may hold values from -6 to 6
- relpos: bfloat16 [128, 128], replicated, may hold values from -4 to 4
- pair_gain: float32 [128], replicated, may hold values from 0.1 to 1.9
- bias_weight: bfloat16 [128, 12], replicated, may hold values from -0.5 to 0.5
- single: float32 [1024, 384], P(('row', 'col')), may hold values from -6 to 6
- rotation_params: float32 [3, 1024], P(None, ('row', 'col')), may hold values from -4 to 4
- translation: float32 [3, 1024], P(None, ('row', 'col')), may hold values from -9 to 9
- residue_index: int32 [1024], P(('row', 'col')), may hold values from 0 to 203776, as said below
- residue_mask: int32 [1024], P(('row', 'col')), may hold values 0 or 1
- w_scalar: float32 [384, 576], replicated, may hold values from -0.3125 to 0.3125
- w_points: float32 [384, 576], replicated, may hold values from -0.3125 to 0.3125
- head_weights: float32 [12], replicated, may hold values from -2 to 1.5
- w_out: float32 [2112, 384], replicated, may hold values from -0.125 to 0.125
- w_hidden: float32 [384, 384], replicated, may hold values from -0.3125 to 0.3125
- w_back: float32 [384, 384], replicated, may hold values from -0.3125 to 0.3125
- w_frame: float32 [384, 6], replicated, may hold values from -0.078125 to 0.078125
Outputs:
- single_out: float32 [1024, 384], P(('row', 'col'))
- frames: float32 [12, 1024], P(None, ('row', 'col'))
Inputs may be any that keep to these rules, and one draw needn't show every extreme that they name: residue_index is strictly increasing along the crop, begins at 0 and ends at exactly 203776.
All inputs are finite; a program needn't handle non-finite values. No bound on the sum of `residue_mask` on one device may be relied on, other than what follows from the above.
Results may differ from a plain program's by a relative error of at most 0.0025.
Values may be sent and summed in bfloat16 or wider, within the bound.
A program may use at most 64 MiB of HBM per device.

v0:
```python
import math
import jax
import jax.numpy as jnp
from jax import lax
from jax.sharding import PartitionSpec as P

H = 12
C = 16
PQ = 4
PV = 8
BINS = 128
ITERS = 3
NORM_EPSILON = 1e-05
MASKED_LOGIT = -100000.0
NORM_FLOOR = 0.1
HIGHEST_PRECISION = lax.Precision.HIGHEST


def rows_first(arrays, axis, dims):
    turned = [jnp.moveaxis(a, dim, 0) for a, dim in zip(arrays, dims)]
    both = jnp.concatenate([t.reshape(len(t), -1) for t in turned], axis=1)
    whole, at, outs = (lax.all_gather(both, axis, axis=0, tiled=True), 0, [])
    for t, dim in zip(turned, dims):
        piece = whole[:, at : at + t[0].size].reshape(-1, *t.shape[1:])
        outs.append(jnp.moveaxis(piece, 0, dim))
        at += t[0].size
    return tuple(outs)


def in_order(parts, dim):
    shape = list(parts.shape[1:])
    shape[dim] *= parts.shape[0]
    return jnp.moveaxis(parts, 0, dim).reshape(shape)


def copy_for_each(value, axis):
    copies = jnp.broadcast_to(value, (lax.axis_size(axis), *value.shape))
    return lax.all_to_all(copies, axis, split_axis=0, concat_axis=0, tiled=True)


def gather_directly(value, axis, dim):
    return in_order(copy_for_each(value, axis), dim)


def broadcast(value, axis, root):
    return lax.dynamic_index_in_dim(lax.all_gather(value, axis), root, 0, keepdims=False)


def of_everyone(value, axis):
    return copy_for_each(value, axis).max(axis=0)


def sent_together(arrays, axis, dim, along):
    both = jnp.concatenate(arrays, axis=along)
    whole, at, outs = (lax.psum_scatter(both, axis, scatter_dimension=dim, tiled=True), 0, [])
    for a in arrays:
        outs.append(lax.slice_in_dim(whole, at, at + a.shape[along], axis=along))
        at += a.shape[along]
    return tuple(outs)


def layer_norm(values):
    center = values - jnp.mean(values, axis=-1, keepdims=True)
    spread = jnp.mean(center * center, axis=-1, keepdims=True)
    return center * lax.rsqrt(spread + NORM_EPSILON)


def rotation_from(update):
    quat_b, quat_c, quat_d = (update[0], update[1], update[2])
    inverse = 1.0 / (1.0 + quat_b * quat_b + quat_c * quat_c + quat_d * quat_d)
    entries = [
        1.0 + quat_b * quat_b - quat_c * quat_c - quat_d * quat_d,
        2.0 * (quat_b * quat_c - quat_d),
        2.0 * (quat_b * quat_d + quat_c),
        2.0 * (quat_b * quat_c + quat_d),
        1.0 - quat_b * quat_b + quat_c * quat_c - quat_d * quat_d,
        2.0 * (quat_c * quat_d - quat_b),
        2.0 * (quat_b * quat_d - quat_c),
        2.0 * (quat_c * quat_d + quat_b),
        1.0 - quat_b * quat_b - quat_c * quat_c + quat_d * quat_d,
    ]
    return jnp.stack(entries) * inverse


def to_global(rotation, points, translation):
    return jnp.stack(
        [
            rotation[3 * component] * points[0]
            + rotation[3 * component + 1] * points[1]
            + rotation[3 * component + 2] * points[2]
            + translation[component]
            for component in range(3)
        ]
    )


def to_local(rotation, points, translation):
    moved = [points[component] - translation[component] for component in range(3)]
    return jnp.stack(
        [
            rotation[component] * moved[0]
            + rotation[3 + component] * moved[1]
            + rotation[6 + component] * moved[2]
            for component in range(3)
        ]
    )


def compose(rotation, translation, update):
    turn = rotation_from(update[:3])
    new_rotation = jnp.stack(
        [
            rotation[3 * left] * turn[right]
            + rotation[3 * left + 1] * turn[3 + right]
            + rotation[3 * left + 2] * turn[6 + right]
            for left in range(3)
            for right in range(3)
        ]
    )
    new_translation = jnp.stack(
        [
            rotation[3 * left] * update[3]
            + rotation[3 * left + 1] * update[4]
            + rotation[3 * left + 2] * update[5]
            + translation[left]
            for left in range(3)
        ]
    )
    return (new_rotation, new_translation)


def project(single, rotation, translation, w_scalar, w_points):
    count = single.shape[0]
    scalars = jnp.dot(
        single, w_scalar, precision=HIGHEST_PRECISION, preferred_element_type=jnp.float32
    ).T
    scalars = scalars.reshape(3, H * C, count).astype(jnp.bfloat16)
    points = jnp.dot(
        single, w_points, precision=HIGHEST_PRECISION, preferred_element_type=jnp.float32
    ).T
    query_local = points[: 3 * H * PQ].reshape(3, H * PQ, count)
    key_local = points[3 * H * PQ : 6 * H * PQ].reshape(3, H * PQ, count)
    value_local = points[6 * H * PQ :].reshape(3, H * PV, count)
    return (
        scalars,
        to_global(rotation, query_local, translation),
        to_global(rotation, key_local, translation),
        to_global(rotation, value_local, translation),
    )


def advance(
    single, rotation, translation, scalar_out, point_out, pair_out, w_out, w_hidden, w_back, w_frame
):
    count = single.shape[0]
    local = to_local(rotation, point_out, translation)
    lengths = jnp.sqrt(jnp.sum(local * local, axis=0) + NORM_FLOOR)
    features = jnp.concatenate(
        [scalar_out, local.reshape(3 * H * PV, count), lengths, pair_out], axis=0
    )
    mixed = jnp.dot(
        features.T, w_out, precision=HIGHEST_PRECISION, preferred_element_type=jnp.float32
    )
    single = layer_norm(single + mixed)
    hidden = jax.nn.relu(
        jnp.dot(single, w_hidden, precision=HIGHEST_PRECISION, preferred_element_type=jnp.float32)
    )
    single = layer_norm(
        single
        + jnp.dot(hidden, w_back, precision=HIGHEST_PRECISION, preferred_element_type=jnp.float32)
    )
    update = jnp.dot(
        single, w_frame, precision=HIGHEST_PRECISION, preferred_element_type=jnp.float32
    ).T
    rotation, translation = compose(rotation, translation, update)
    return (single, rotation, translation)


def attend_block(
    query, keyval, query_side, key_side, value_side, bias, normed, pair_live, point_scale
):
    heads_query = query.reshape(H, C, -1)
    keys = keyval[0].reshape(H, C, -1)
    values = keyval[1].reshape(H, C, -1)
    query_grid = query_side.reshape(3, H, PQ, -1)
    key_grid = key_side.reshape(3, H, PQ, -1)
    value_grid = value_side.reshape(3, H, PV, -1)
    scores = jnp.einsum(
        "hci,hcj->hij", heads_query, keys, preferred_element_type=jnp.float32
    ) / math.sqrt(C)
    cross = jnp.einsum("ahpi,ahpj->hij", query_grid, key_grid, precision=HIGHEST_PRECISION)
    distance = (
        jnp.sum(query_grid * query_grid, axis=(0, 2))[:, :, None]
        + jnp.sum(key_grid * key_grid, axis=(0, 2))[:, None, :]
        - 2.0 * cross
    )
    logits = math.sqrt(1.0 / 3.0) * (scores + bias - point_scale[:, None, None] * distance)
    logits = jnp.where(pair_live[None], logits, MASKED_LOGIT)
    local_max = jnp.max(logits, axis=-1)
    unscaled = jnp.exp(logits - local_max[:, :, None])
    total_weight = jnp.sum(unscaled, axis=-1)
    rounded = unscaled.astype(jnp.bfloat16)
    scalar_sum = jnp.einsum("hij,hcj->hci", rounded, values, preferred_element_type=jnp.float32)
    point_sum = jnp.einsum("hij,ahpj->ahpi", unscaled, value_grid, precision=HIGHEST_PRECISION)
    pair_sum = jnp.einsum("hij,ijc->hci", rounded, normed, preferred_element_type=jnp.float32)
    return (local_max, total_weight, scalar_sum, point_sum, pair_sum)


def body(
    pair,
    relpos,
    pair_gain,
    bias_weight,
    single,
    rotation_params,
    translation,
    residue_index,
    residue_mask,
    w_scalar,
    w_points,
    head_weights,
    w_out,
    w_hidden,
    w_back,
    w_frame,
):
    row_rows = pair.shape[0]
    col_rows = pair.shape[1]
    owned = single.shape[0]
    row_place = lax.axis_index("row")
    col_place = lax.axis_index("col")
    index_all, mask_all = rows_first((residue_index, residue_mask), ("row", "col"), (0, 0))
    query_index = lax.dynamic_slice_in_dim(index_all, row_place * row_rows, row_rows, 0)
    key_index = lax.dynamic_slice_in_dim(index_all, col_place * col_rows, col_rows, 0)
    query_live = lax.dynamic_slice_in_dim(mask_all, row_place * row_rows, row_rows, 0) == 1
    key_live = lax.dynamic_slice_in_dim(mask_all, col_place * col_rows, col_rows, 0) == 1
    pair_live = query_live[:, None] & key_live[None, :]
    span_rows = math.gcd(row_rows, 64)

    def prepare(index):
        offset = (
            jnp.clip(key_index[None, :] - query_index[:, None], -(BINS // 2), BINS // 2 - 1)
            + BINS // 2
        )
        onehot = (offset[:, :, None] == lax.broadcasted_iota(jnp.int32, (1, 1, BINS), 2)).astype(
            jnp.bfloat16
        )
        embedded = jnp.dot(
            onehot.reshape(span_rows * col_rows, BINS), relpos, preferred_element_type=jnp.float32
        )
        summed = pair.astype(jnp.float32) + embedded.reshape(span_rows, col_rows, -1)
        normed_part = (layer_norm(summed) * pair_gain).astype(jnp.bfloat16)
        bias_part = jnp.einsum(
            "ijc,ch->hij", normed_part, bias_weight, preferred_element_type=jnp.float32
        )
        return (normed_part, bias_part)

    normed_blocks, bias_blocks = lax.map(
        prepare, jnp.arange(row_rows // span_rows, dtype=jnp.int32)
    )
    normed = normed_blocks.reshape(row_rows, col_rows, -1)
    bias = bias_blocks.transpose(1, 0, 2, 3).reshape(H, row_rows, col_rows)
    point_scale = jax.nn.softplus(head_weights) * (math.sqrt(2.0 / (9.0 * PQ)) / 2.0)
    rotation = rotation_from(rotation_params)
    state = single
    for step in range(ITERS):
        scalars, query_points, key_points, value_points = project(
            state, rotation, translation, w_scalar, w_points
        )
        query_flat = query_points.reshape(-1, owned)
        key_flat = key_points.reshape(-1, owned)
        value_flat = value_points.reshape(-1, owned)
        block_scalar = gather_directly(scalars, "col", 2)
        block_point = rows_first((query_flat, key_flat, value_flat), "col", (1, 1, 1))
        query = block_scalar[0]
        query_side = block_point[0]
        ratio = lax.axis_size("row") // lax.axis_size("col")
        scalar_pieces = []
        key_pieces = []
        value_pieces = []
        for part in range(ratio):
            root = col_place * ratio + part
            scalar_pieces.append(broadcast(block_scalar[1:], "row", root))
            key_piece, value_piece = (
                broadcast(block_point[1], "row", root),
                broadcast(block_point[2], "row", root),
            )
            key_pieces.append(key_piece)
            value_pieces.append(value_piece)
        keyval = jnp.concatenate(scalar_pieces, axis=2)
        key_side = jnp.concatenate(key_pieces, axis=1)
        value_side = jnp.concatenate(value_pieces, axis=1)
        local_max, total_weight, scalar_sum, point_sum, pair_sum = attend_block(
            query, keyval, query_side, key_side, value_side, bias, normed, pair_live, point_scale
        )
        pair_out = None
        row_top = of_everyone(local_max, "col")
        factor = jnp.exp(local_max - row_top)
        shares = sent_together(
            (
                total_weight * factor,
                (scalar_sum * factor[:, None, :]).reshape(H * C, row_rows),
                (point_sum * factor[None, :, None, :]).reshape(3 * H * PV, row_rows),
                (pair_sum * factor[:, None, :]).reshape(-1, row_rows),
            ),
            "col",
            1,
            0,
        )
        total = shares[0]
        scalar_out = (shares[1].reshape(H, C, owned) / total[:, None, :]).reshape(H * C, owned)
        point_out = (shares[2].reshape(3, H, PV, owned) / total[None, :, None, :]).reshape(
            3, H * PV, owned
        )
        pair_out = (shares[3].reshape(H, -1, owned) / total[:, None, :]).reshape(-1, owned)
        state, rotation, translation = advance(
            state,
            rotation,
            translation,
            scalar_out,
            point_out,
            pair_out,
            w_out,
            w_hidden,
            w_back,
            w_frame,
        )
    frames = jnp.concatenate([rotation, translation], axis=0)
    return (state, frames)


def solution(mesh):
    placed = (
        P("row", "col", None),
        P(),
        P(),
        P(),
        P(("row", "col"), None),
        P(None, ("row", "col")),
        P(None, ("row", "col")),
        P(("row", "col")),
        P(("row", "col")),
        P(),
        P(),
        P(),
        P(),
        P(),
        P(),
        P(),
    )
    return jax.shard_map(
        body,
        mesh=mesh,
        in_specs=placed,
        out_specs=(P(("row", "col"), None), P(None, ("row", "col"))),
        check_vma=False,
    )
```

profile of v0, /device:TPU:0, one launch (start us, length us, event | category | flops | bytes accessed | tf_op | source)
XLA Modules:
  0.0 859.4 jit_solution(4518014439812937433)
XLA Ops:
  7.2 2.2 convolution_convert_fusion.2
  10.1 5.4 all-to-all-start
  17.2 2.0 fusion.105
  21.4 29.0 %all_gather.87 = f32[64,576]{1,0:T(8,128)S(1)} all-gather(f32[8,576]{1,0:T(8,128)S(1)} %pad_maximum_fusion.9), channel_id=1, replica_groups=mesh['row'=16,'col'=8] {'col'}, dimensions={0}, use_global_device_ids=true | all-gather | bytes 165888 | tf_op jit(solution)/shard_map/all_gather | solution.py:22
  51.9 311.7 %all-gather.6 = s32[128,8,2]{1,2,0:T(2,128)S(1)} all-gather(s32[1,8,2]{1,2,0:T(2,128)S(1)} %add_bitcast_fusion.27), channel_id=1, replica_groups=mesh['row'=16,'col'=8] {'row','col'}, dimensions={0}, use_global_device_ids=true | all-gather | bytes 8256 | tf_op jit(solution)/shard_map/all_gather | solution.py:22
  363.9 4.1 copy.370
  368.1 3.8 fusion.95
  371.9 2.0 copy-done.2
  375.8 24.2 %all-gather.7 = f32[16,144,64]{1,2,0:T(8,128)} all-gather(f32[1,144,64]{1,2,0:T(8,128)} %get-tuple-element.84), channel_id=2, replica_groups=mesh['row'=16,'col'=8] {'row'}, dimensions={0}, use_global_device_ids=true | all-gather | bytes 626688 | tf_op jit(solution)/shard_map/all_gather | solution.py:46
  400.0 1.5 constant_dynamic-slice_fusion.11
  401.5 1.6 copy.462
  403.0 1.6 copy.461
  405.2 3.2 multiply_convert_fusion
  408.3 1.3 copy-done.1
  413.5 23.1 %all_gather.86 = bf16[16,2,192,64]{2,3,1,0:T(8,128)(2,1)S(1)} all-gather(bf16[1,2,192,64]{2,3,1,0:T(8,128)(2,1)S(1)} %slice_bitcast_fusion.11), channel_id=1, replica_groups=mesh['row'=16,'col'=8] {'row'}, dimensions={0}, use_global_device_ids=true | all-gather | bytes 835584 | tf_op jit(solution)/shard_map/all_gather | solution.py:46
  439.7 2.7 fusion.96
  443.1 3.3 all-to-all-start.1
  446.7 1.3 fusion.34
  448.0 1.6 copy.381
  449.5 3.0 all-to-all-done.1
  457.0 2.8 fusion.2
  460.7 1.6 constant_dynamic-slice_fusion.9
  463.4 1.8 fusion.28
  465.5 2.1 concatenate.99
  467.6 33.0 %reduce-scatter.4.cloned.1.call-done = f32[2028,8]{0,1:T(8,128)} async-done(((f32[2028,64]{0,1:T(8,128)}), f32[2028,8]{0,1:T(8,128)}) %reduce-scatter.4.cloned.1.call-update) | async-done | bytes 64912 | tf_op jit(solution)/shard_map/reduce_scatter | solution.py:55
  505.0 1.8 fusion.97
  511.3 28.2 %all_gather.94 = f32[64,576]{1,0:T(8,128)S(1)} all-gather(f32[8,576]{1,0:T(8,128)S(1)} %pad_maximum_fusion.10), channel_id=1, replica_groups=mesh['row'=16,'col'=8] {'col'}, dimensions={0}, use_global_device_ids=true | all-gather | bytes 165888 | tf_op jit(solution)/shard_map/all_gather | solution.py:22
  541.7 3.4 all-to-all-start.2
  546.1 26.9 %all-gather.9 = f32[16,144,64]{1,2,0:T(8,128)S(1)} all-gather(f32[1,144,64]{1,2,0:T(8,128)S(1)} %get-tuple-element.82), channel_id=4, replica_groups=mesh['row'=16,'col'=8] {'row'}, dimensions={0}, use_global_device_ids=true | all-gather | bytes 626688 | tf_op jit(solution)/shard_map/all_gather | solution.py:46
  574.6 1.6 copy.465
  576.2 1.6 multiply_reduce_fusion.3
  578.5 22.4 %all_gather.93 = bf16[16,2,192,64]{2,3,1,0:T(8,128)(2,1)S(1)} all-gather(bf16[1,2,192,64]{2,3,1,0:T(8,128)(2,1)S(1)} %slice_bitcast_fusion.8), channel_id=1, replica_groups=mesh['row'=16,'col'=8] {'row'}, dimensions={0}, use_global_device_ids=true | all-gather | bytes 835584 | tf_op jit(solution)/shard_map/all_gather | solution.py:46
  602.5 1.3 fusion.8
  603.8 2.7 fusion.99
  607.2 5.2 all-to-all-start.3
  612.7 1.9 fusion.36
  614.6 1.6 copy.406
  616.2 2.5 all-to-all-done.3
  618.7 1.3 reduce.1
  624.6 2.8 fusion.3
  628.3 1.6 constant_dynamic-slice_fusion.5
  631.0 1.8 fusion.27
  633.0 2.1 concatenate.109
  635.1 35.0 %reduce-scatter.6.cloned.1.call-done = f32[2028,8]{0,1:T(8,128)} async-done(((f32[2028,64]{0,1:T(8,128)}), f32[2028,8]{0,1:T(8,128)}) %reduce-scatter.6.cloned.1.call-update) | async-done | bytes 64912 | tf_op jit(solution)/shard_map/reduce_scatter | solution.py:55
  675.2 2.6 fusion.100
  682.4 28.2 %all_gather.101 = f32[64,576]{1,0:T(8,128)S(1)} all-gather(f32[8,576]{1,0:T(8,128)S(1)} %pad_maximum_fusion.11), channel_id=1, replica_groups=mesh['row'=16,'col'=8] {'col'}, dimensions={0}, use_global_device_ids=true | all-gather | bytes 165888 | tf_op jit(solution)/shard_map/all_gather | solution.py:22
  712.8 3.4 all-to-all-start.4
  717.2 26.9 %all-gather.11 = f32[16,144,64]{1,2,0:T(8,128)S(1)} all-gather(f32[1,144,64]{1,2,0:T(8,128)S(1)} %get-tuple-element.80), channel_id=6, replica_groups=mesh['row'=16,'col'=8] {'row'}, dimensions={0}, use_global_device_ids=true | all-gather | bytes 626688 | tf_op jit(solution)/shard_map/all_gather | solution.py:46
  745.6 1.6 copy.469
  747.3 1.6 multiply_reduce_fusion.1
  749.6 22.4 %all_gather.100 = bf16[16,2,192,64]{2,3,1,0:T(8,128)(2,1)S(1)} all-gather(bf16[1,2,192,64]{2,3,1,0:T(8,128)(2,1)S(1)} %slice_bitcast_fusion.5), channel_id=1, replica_groups=mesh['row'=16,'col'=8] {'row'}, dimensions={0}, use_global_device_ids=true | all-gather | bytes 835584 | tf_op jit(solution)/shard_map/all_gather | solution.py:46
  773.6 1.3 fusion.11
  774.9 2.7 fusion.102
  778.3 5.2 all-to-all-start.5
  783.8 1.9 fusion.38
  785.7 1.6 copy.431
  787.3 2.4 all-to-all-done.5
  789.7 1.3 reduce.2
  795.7 2.8 fusion.4
  799.3 1.6 constant_dynamic-slice_fusion.1
  802.0 1.8 fusion.26
  804.0 2.1 concatenate.119
  806.2 35.0 %reduce-scatter.8.cloned.1.call-done = f32[2028,8]{0,1:T(8,128)} async-done(((f32[2028,64]{0,1:T(8,128)}), f32[2028,8]{0,1:T(8,128)}) %reduce-scatter.8.cloned.1.call-update) | async-done | bytes 64912 | tf_op jit(solution)/shard_map/reduce_scatter | solution.py:55
  846.1 2.5 fusion.103
  (504 shorter events, 78.9 us)
Async XLA Ops:
  7.2 497.7 %copy-start = (f32[2112,384]{1,0:T(8,128)S(1)}, f32[2112,384]{1,0:T(8,128)}, u32[]{:S(2)}) copy-start(f32[2112,384]{1,0:T(8,128)} %param.28) | copy-start | bytes 9732100
  7.2 44.7 %copy-start.105 = (s32[8]{0:T(128)S(1)}, s32[8]{0:T(128)}, u32[]{:S(2)}) copy-start(s32[8]{0:T(128)} %param.24) | copy-start | bytes 100
  7.2 44.7 %copy-start.106 = (s32[8]{0:T(128)S(1)}, s32[8]{0:T(128)}, u32[]{:S(2)}) copy-start(s32[8]{0:T(128)} %param.23) | copy-start | bytes 100
  10.1 402.7 %all-to-all-start = ((bf16[8,3,192,8]{2,3,1,0:T(8,128)(2,1)}), bf16[8,3,192,8]{2,3,1,0:T(8,128)(2,1)S(1)}, u32[]{:S(2)}, u32[]{:S(2)}) async-start(bf16[8,3,192,8]{2,3,1,0:T(8,128)(2,1)} %broadcast_in_dim.51), calls=%async_computation | async-start | bytes 196608 | tf_op jit(solution)/shard_map/all_to_all | solution.py:38
  15.6 445.1 %all-gather.17.cloned.1.call-start = ((), (), s32[]{:S(2)}) async-start(), calls=%async_computation.12 | async-start | bytes 1671168 | tf_op jit(solution)/shard_map/all_gather | solution.py:46
  19.2 348.8 %copy-start.28 = (bf16[128,128]{1,0:T(8,128)(2,1)S(1)}, bf16[128,128]{1,0:T(8,128)(2,1)}, u32[]{:S(2)}) copy-start(bf16[128,128]{1,0:T(8,128)(2,1)} %param.17) | copy-start | bytes 98308
  371.9 32.7 %copy-start.107 = (f32[12]{0:T(128)S(1)}, f32[12]{0:T(128)}, u32[]{:S(2)}) copy-start(f32[12]{0:T(128)} %param.27) | copy-start | bytes 148
  371.9 33.2 %copy-start.104 = (f32[128]{0:T(128)S(1)}, f32[128]{0:T(128)}, u32[]{:S(2)}) copy-start(f32[128]{0:T(128)} %param.18) | copy-start | bytes 1540
  375.8 36.5 %copy-start.13 = (f32[144,64]{1,0:T(8,128)}, f32[144,64]{1,0:T(8,128)S(1)}, u32[]{:S(2)}) copy-start(f32[144,64]{1,0:T(8,128)S(1)} %copy.377) | copy-start | bytes 110596
  403.0 6.6 copy-start.103
  443.1 9.5 %all-to-all-start.1 = ((f32[8,1,768]{2,1,0:T(1,128)}), f32[8,1,768]{2,1,0:T(1,128)S(1)}, u32[]{:S(2)}, u32[]{:S(2)}) async-start(f32[8,1,768]{2,1,0:T(1,128)} %reshape.2142), calls=%async_computation.1 | async-start | bytes 49152 | tf_op jit(solution)/shard_map/all_to_all | solution.py:38
  446.4 54.1 %reduce-scatter.4.cloned.1.call-start = ((), (), s32[]{:S(2)}) async-start(), calls=%async_computation.9 | async-start | bytes 589824 | tf_op jit(solution)/shard_map/reduce_scatter | solution.py:55
  465.2 37.5 %copy-start.75 = (f32[8]{0:T(128)S(1)}, f32[8]{0:T(128)}, u32[]{:S(2)}) copy-start(f32[8]{0:T(128)} %copy-done.74) | copy-start | bytes 100
  465.2 37.6 %copy-start.77 = (f32[8]{0:T(128)S(1)}, f32[8]{0:T(128)}, u32[]{:S(2)}) copy-start(f32[8]{0:T(128)} %copy-done.76) | copy-start | bytes 100
  465.2 37.6 %copy-start.79 = (f32[8]{0:T(128)S(1)}, f32[8]{0:T(128)}, u32[]{:S(2)}) copy-start(f32[8]{0:T(128)} %copy-done.78) | copy-start | bytes 100
  465.3 37.6 %copy-start.81 = (f32[8]{0:T(128)S(1)}, f32[8]{0:T(128)}, u32[]{:S(2)}) copy-start(f32[8]{0:T(128)} %copy-done.80) | copy-start | bytes 100
  465.3 37.6 %copy-start.83 = (f32[8]{0:T(128)S(1)}, f32[8]{0:T(128)}, u32[]{:S(2)}) copy-start(f32[8]{0:T(128)} %copy-done.82) | copy-start | bytes 100
  465.3 37.6 %copy-start.85 = (f32[8]{0:T(128)S(1)}, f32[8]{0:T(128)}, u32[]{:S(2)}) copy-start(f32[8]{0:T(128)} %copy-done.84) | copy-start | bytes 100
  465.3 37.6 %copy-start.87 = (f32[8]{0:T(128)S(1)}, f32[8]{0:T(128)}, u32[]{:S(2)}) copy-start(f32[8]{0:T(128)} %copy-done.86) | copy-start | bytes 100
  465.3 37.6 %copy-start.89 = (f32[8]{0:T(128)S(1)}, f32[8]{0:T(128)}, u32[]{:S(2)}) copy-start(f32[8]{0:T(128)} %copy-done.88) | copy-start | bytes 100
  465.3 37.6 %copy-start.91 = (f32[8]{0:T(128)S(1)}, f32[8]{0:T(128)}, u32[]{:S(2)}) copy-start(f32[8]{0:T(128)} %copy-done.90) | copy-start | bytes 100
  465.3 37.6 %copy-start.93 = (f32[8]{0:T(128)S(1)}, f32[8]{0:T(128)}, u32[]{:S(2)}) copy-start(f32[8]{0:T(128)} %copy-done.92) | copy-start | bytes 100
  465.3 37.6 %copy-start.95 = (f32[8]{0:T(128)S(1)}, f32[8]{0:T(128)}, u32[]{:S(2)}) copy-start(f32[8]{0:T(128)} %copy-done.94) | copy-start | bytes 100
  465.3 37.6 %copy-start.97 = (f32[8]{0:T(128)S(1)}, f32[8]{0:T(128)}, u32[]{:S(2)}) copy-start(f32[8]{0:T(128)} %copy-done.96) | copy-start | bytes 100
  465.3 39.6 %copy-start.24 = (f32[8,384]{1,0:T(8,128)S(1)}, f32[8,384]{1,0:T(8,128)}, u32[]{:S(2)}) copy-start(f32[8,384]{1,0:T(8,128)} %param.20) | copy-start | bytes 36868
  510.2 31.5 %copy-start.63 = (f32[1,8]{1,0:T(1,128)}, f32[1,8]{1,0:T(1,128)S(1)}, u32[]{:S(2)}) copy-start(f32[1,8]{1,0:T(1,128)S(1)} %get-tuple-element.125) | copy-start | bytes 100
  510.4 31.3 %copy-start.59 = (f32[1,8]{1,0:T(1,128)}, f32[1,8]{1,0:T(1,128)S(1)}, u32[]{:S(2)}) copy-start(f32[1,8]{1,0:T(1,128)S(1)} %get-tuple-element.117) | copy-start | bytes 100
  541.7 36.8 %all-to-all-start.2 = ((bf16[8,3,192,8]{2,3,1,0:T(8,128)(2,1)}), bf16[8,3,192,8]{2,3,1,0:T(8,128)(2,1)S(1)}, u32[]{:S(2)}, u32[]{:S(2)}) async-start(bf16[8,3,192,8]{2,3,1,0:T(8,128)(2,1)} %broadcast_in_dim.54), calls=%async_computation.3 | async-start | bytes 196608 | tf_op jit(solution)/shard_map/all_to_all | solution.py:38
  545.1 83.3 %all-gather.19.cloned.1.call-start = ((), (), s32[]{:S(2)}) async-start(), calls=%async_computation.13 | async-start | bytes 1671168 | tf_op jit(solution)/shard_map/all_gather | solution.py:46
  546.1 55.5 %copy-start.15 = (f32[144,64]{1,0:T(8,128)}, f32[144,64]{1,0:T(8,128)S(1)}, u32[]{:S(2)}) copy-start(f32[144,64]{1,0:T(8,128)S(1)} %copy.402) | copy-start | bytes 110596
  574.6 27.0 %copy-start.19 = (f32[1,144,64]{2,1,0:T(8,128)}, f32[1,144,64]{2,1,0:T(8,128)S(1)}, u32[]{:S(2)}) copy-start(f32[1,144,64]{2,1,0:T(8,128)S(1)} %copy.466) | copy-start | bytes 110596
  606.5 16.4 %copy-start.21 = (f32[12,64]{1,0:T(8,128)}, f32[12,64]{1,0:T(8,128)S(1)}, u32[]{:S(2)}) copy-start(f32[12,64]{1,0:T(8,128)S(1)} %get-tuple-element.229) | copy-start | bytes 9220
  607.2 11.5 %all-to-all-start.3 = ((f32[8,1,768]{2,1,0:T(1,128)}), f32[8,1,768]{2,1,0:T(1,128)S(1)}, u32[]{:S(2)}, u32[]{:S(2)}) async-start(f32[8,1,768]{2,1,0:T(1,128)} %reshape.2144), calls=%async_computation.4 | async-start | bytes 49152 | tf_op jit(solution)/shard_map/all_to_all | solution.py:38
  612.4 57.7 %reduce-scatter.6.cloned.1.call-start = ((), (), s32[]{:S(2)}) async-start(), calls=%async_computation.10 | async-start | bytes 589824 | tf_op jit(solution)/shard_map/reduce_scatter | solution.py:55
  675.1 6.0 copy-start.30
  675.1 6.0 copy-start.54
  675.1 6.0 copy-start.56
  675.2 6.0 copy-start.66
  675.2 6.1 copy-start.32
  675.2 6.1 copy-start.58
  675.2 6.1 copy-start.60
  675.2 6.1 copy-start.64
  681.3 31.5 %copy-start.69 = (f32[1,8]{1,0:T(1,128)}, f32[1,8]{1,0:T(1,128)S(1)}, u32[]{:S(2)}) copy-start(f32[1,8]{1,0:T(1,128)S(1)} %get-tuple-element.184) | copy-start | bytes 100
  681.4 68.1 %copy-start.41 = (f32[1,8]{1,0:T(1,128)}, f32[1,8]{1,0:T(1,128)S(1)}, u32[]{:S(2)}) copy-start(f32[1,8]{1,0:T(1,128)S(1)} %get-tuple-element.157) | copy-start | bytes 100
  681.5 68.0 %copy-start.47 = (f32[1,8]{1,0:T(1,128)}, f32[1,8]{1,0:T(1,128)S(1)}, u32[]{:S(2)}) copy-start(f32[1,8]{1,0:T(1,128)S(1)} %get-tuple-element.154) | copy-start | bytes 100
  681.5 68.0 %copy-start.49 = (f32[1,8]{1,0:T(1,128)}, f32[1,8]{1,0:T(1,128)S(1)}, u32[]{:S(2)}) copy-start(f32[1,8]{1,0:T(1,128)S(1)} %get-tuple-element.155) | copy-start | bytes 100
  681.5 68.0 %copy-start.51 = (f32[1,8]{1,0:T(1,128)}, f32[1,8]{1,0:T(1,128)S(1)}, u32[]{:S(2)}) copy-start(f32[1,8]{1,0:T(1,128)S(1)} %get-tuple-element.156) | copy-start | bytes 100
  712.8 36.7 %all-to-all-start.4 = ((bf16[8,3,192,8]{2,3,1,0:T(8,128)(2,1)}), bf16[8,3,192,8]{2,3,1,0:T(8,128)(2,1)S(1)}, u32[]{:S(2)}, u32[]{:S(2)}) async-start(bf16[8,3,192,8]{2,3,1,0:T(8,128)(2,1)} %broadcast_in_dim.56), calls=%async_computation.6 | async-start | bytes 196608 | tf_op jit(solution)/shard_map/all_to_all | solution.py:38
  716.2 83.2 %all-gather.21.cloned.1.call-start = ((), (), s32[]{:S(2)}) async-start(), calls=%async_computation.14 | async-start | bytes 1671168 | tf_op jit(solution)/shard_map/all_gather | solution.py:46
  717.2 55.5 %copy-start.14 = (f32[144,64]{1,0:T(8,128)}, f32[144,64]{1,0:T(8,128)S(1)}, u32[]{:S(2)}) copy-start(f32[144,64]{1,0:T(8,128)S(1)} %copy.427) | copy-start | bytes 110596
  745.6 27.0 %copy-start.17 = (f32[1,144,64]{2,1,0:T(8,128)}, f32[1,144,64]{2,1,0:T(8,128)S(1)}, u32[]{:S(2)}) copy-start(f32[1,144,64]{2,1,0:T(8,128)S(1)} %copy.470) | copy-start | bytes 110596
  777.6 16.4 %copy-start.20 = (f32[12,64]{1,0:T(8,128)}, f32[12,64]{1,0:T(8,128)S(1)}, u32[]{:S(2)}) copy-start(f32[12,64]{1,0:T(8,128)S(1)} %get-tuple-element.235) | copy-start | bytes 9220
  778.3 11.4 %all-to-all-start.5 = ((f32[8,1,768]{2,1,0:T(1,128)}), f32[8,1,768]{2,1,0:T(1,128)S(1)}, u32[]{:S(2)}, u32[]{:S(2)}) async-start(f32[8,1,768]{2,1,0:T(1,128)} %reshape.2146), calls=%async_computation.7 | async-start | bytes 49152 | tf_op jit(solution)/shard_map/all_to_all | solution.py:38
  783.5 57.7 %reduce-scatter.8.cloned.1.call-start = ((), (), s32[]{:S(2)}) async-start(), calls=%async_computation.11 | async-start | bytes 589824 | tf_op jit(solution)/shard_map/reduce_scatter | solution.py:55
  806.1 44.8 %copy-start.48 = (f32[1,8]{1,0:T(1,128)S(1)}, f32[1,8]{1,0:T(1,128)}, u32[]{:S(2)}) copy-start(f32[1,8]{1,0:T(1,128)} %copy-done.47) | copy-start | bytes 100
  806.1 44.8 %copy-start.50 = (f32[1,8]{1,0:T(1,128)S(1)}, f32[1,8]{1,0:T(1,128)}, u32[]{:S(2)}) copy-start(f32[1,8]{1,0:T(1,128)} %copy-done.49) | copy-start | bytes 100
  806.1 44.8 %copy-start.52 = (f32[1,8]{1,0:T(1,128)S(1)}, f32[1,8]{1,0:T(1,128)}, u32[]{:S(2)}) copy-start(f32[1,8]{1,0:T(1,128)} %copy-done.51) | copy-start | bytes 100
  841.8 9.8 %copy-start.34 = (f32[1,8]{1,0:T(1,128)S(1)}, f32[1,8]{1,0:T(1,128)}, u32[]{:S(2)}) copy-start(f32[1,8]{1,0:T(1,128)} %copy-done.33) | copy-start | bytes 100
  841.8 9.8 %copy-start.36 = (f32[1,8]{1,0:T(1,128)S(1)}, f32[1,8]{1,0:T(1,128)}, u32[]{:S(2)}) copy-start(f32[1,8]{1,0:T(1,128)} %copy-done.35) | copy-start | bytes 100
  841.8 9.8 %copy-start.70 = (f32[1,8]{1,0:T(1,128)S(1)}, f32[1,8]{1,0:T(1,128)}, u32[]{:S(2)}) copy-start(f32[1,8]{1,0:T(1,128)} %copy-done.69) | copy-start | bytes 100
  841.9 9.7 %copy-start.42 = (f32[1,8]{1,0:T(1,128)S(1)}, f32[1,8]{1,0:T(1,128)}, u32[]{:S(2)}) copy-start(f32[1,8]{1,0:T(1,128)} %copy-done.41) | copy-start | bytes 100
  841.9 9.7 %copy-start.44 = (f32[1,8]{1,0:T(1,128)S(1)}, f32[1,8]{1,0:T(1,128)}, u32[]{:S(2)}) copy-start(f32[1,8]{1,0:T(1,128)} %copy-done.43) | copy-start | bytes 100
  841.9 9.7 %copy-start.46 = (f32[1,8]{1,0:T(1,128)S(1)}, f32[1,8]{1,0:T(1,128)}, u32[]{:S(2)}) copy-start(f32[1,8]{1,0:T(1,128)} %copy-done.45) | copy-start | bytes 100
  841.9 9.8 %copy-start.68 = (f32[1,8]{1,0:T(1,128)S(1)}, f32[1,8]{1,0:T(1,128)}, u32[]{:S(2)}) copy-start(f32[1,8]{1,0:T(1,128)} %copy-done.67) | copy-start | bytes 100
  (56 other events, 121.9 us)
Sparse Core Ops, SparseCore 0:
  51.3 47.5 all-gather.16
  467.7 32.7 reduce-scatter.3
  576.4 43.9 all-gather.18
  635.2 34.8 reduce-scatter.5
  747.4 44.0 all-gather.20
  806.2 34.8 reduce-scatter.7
where the time goes:
time: 863 us; the launch traced here: 859 us
  blocking collectives  543 us (63%)
  waiting for transfers between devices  111 us (13%)
  local copies, waits for them, and re-layouts  74.6 us (9%)
  matrix products  52.3 us (6%)
  other arithmetic  35.2 us (4%)
  starting transfers between devices  26.8 us (3%)
  between operations  16.3 us (2%)
    all_gather x4, blocking collectives, rows_first(): whole, at, outs = (lax.all_gather(both, axis, axis=0, tiled=True), 0, [])  397 us
    all_gather x6, blocking collectives, broadcast(): lax.all_gather(value, axis)  146 us
    reduce_scatter x3, waiting for transfers between devices, sent_together(): lax.psum_scatter(both, axis, scatter_dimension=dim, tiled=True)  103 us
    unnamed x246, local copies, waits for them, and re-layouts  31.3 us
    all_to_all x6, starting transfers between devices, copy_for_each(): return lax.all_to_all(copies, axis, split_axis=0, concat_axis=0, tiled=True)  25.9 us
  transfers between devices with their start and end apart: 12, of which 6 were waited for; matrix products, arithmetic and copies ran while one was open for 11% of the time, Pallas kernels for 0%

commit v1 on v0

--- a/solution.py
+++ b/solution.py
@@ -19,7 +19,13 @@
 def rows_first(arrays, axis, dims):
     turned = [jnp.moveaxis(a, dim, 0) for a, dim in zip(arrays, dims)]
     both = jnp.concatenate([t.reshape(len(t), -1) for t in turned], axis=1)
-    whole, at, outs = (lax.all_gather(both, axis, axis=0, tiled=True), 0, [])
+    whole, at, outs = (
+        jnp.concatenate(
+            lax.all_to_all(jnp.stack([both] * lax.axis_size(axis)), axis, 0, 0), axis=0
+        ),
+        0,
+        [],
+    )
     for t, dim in zip(turned, dims):
         piece = whole[:, at : at + t[0].size].reshape(-1, *t.shape[1:])
         outs.append(jnp.moveaxis(piece, 0, dim))

time: 863 us -> 495 us (0.57)
  blocking collectives: 543 us -> 149 us
  starting transfers between devices: 26.8 us -> 52.2 us
  waiting for transfers between devices: 111 us -> 129 us
  local copies, waits for them, and re-layouts: 74.6 us -> 65 us
    all_gather x4 -> x0, blocking collectives: 397 us -> none  [rows_first(): whole, at, outs = (lax.all_gather(both, axis, axis=0, tiled=True), 0, [])]
    all_to_all x0 -> x4, starting transfers between devices: none -> 23.7 us  [rows_first(): lax.all_to_all(jnp.stack([both] * lax.axis_size(axis)), axis, 0, 0)]
    all_to_all x6, waiting for transfers between devices: 7.99 us -> 24.7 us  [copy_for_each(): return lax.all_to_all(copies, axis, split_axis=0, concat_axis=0, tiled=True)]
    unnamed x246 -> x223, local copies, waits for them, and re-layouts: 31.3 us -> 20.4 us
  transfers between devices with their start and end apart: 12 -> 16, of which waited for: 6 -> 8; matrix products, arithmetic and copies ran while one was open for 11% -> 17% of each run, Pallas kernels for 0% -> 0%
where the time goes in v1:
time: 495 us; the launch traced here: 492 us
  blocking collectives  149 us (30%)
  waiting for transfers between devices  129 us (26%)
  local copies, waits for them, and re-layouts  65 us (13%)
  matrix products  54.6 us (11%)
  starting transfers between devices  52.2 us (11%)
  other arithmetic  26.7 us (5%)
  between operations  16.2 us (3%)
    all_gather x6, blocking collectives, broadcast(): lax.all_gather(value, axis)  149 us
    reduce_scatter x3, waiting for transfers between devices, sent_together(): lax.psum_scatter(both, axis, scatter_dimension=dim, tiled=True)  104 us
    all_to_all x6, starting transfers between devices, copy_for_each(): return lax.all_to_all(copies, axis, split_axis=0, concat_axis=0, tiled=True)  27.7 us
    all_to_all x6, waiting for transfers between devices, copy_for_each(): return lax.all_to_all(copies, axis, split_axis=0, concat_axis=0, tiled=True)  24.7 us
    all_to_all x4, starting transfers between devices, rows_first(): lax.all_to_all(jnp.stack([both] * lax.axis_size(axis)), axis, 0, 0)  23.7 us
    unnamed x223, local copies, waits for them, and re-layouts  20.4 us
  transfers between devices with their start and end apart: 16, of which 8 were waited for; matrix products, arithmetic and copies ran while one was open for 17% of the time, Pallas kernels for 0%

profile of v1, /device:TPU:0, one launch (start us, length us, event | category | flops | bytes accessed | tf_op | source)
XLA Modules:
  0.0 492.1 jit_solution(3099421878493681701)
XLA Ops:
  8.7 11.2 %all-to-all-start = ((s32[128,8,2]{1,2,0:T(2,128)}), s32[128,8,2]{1,2,0:T(2,128)S(1)}, u32[]{:S(2)}, u32[]{:S(2)}) async-start(s32[128,8,2]{1,2,0:T(2,128)} %stack.94), calls=%async_computation | async-start | bytes 262144 | tf_op jit(solution)/shard_map/all_to_all | solution.py:24
  21.5 2.0 fusion.105
  25.8 2.0 convolution_convert_fusion.2
  28.1 1.2 fusion.82
  29.5 4.1 copy.359
  34.2 4.6 all-to-all-start.1
  39.3 3.8 fusion.95
  44.9 1.3 copy-done.1
  46.2 1.2 fusion.80
  48.1 5.7 %all-to-all-start.2 = ((f32[8,8,576]{2,1,0:T(8,128)}), f32[8,8,576]{2,1,0:T(8,128)S(1)}, u32[]{:S(2)}, u32[]{:S(2)}) async-start(f32[8,8,576]{2,1,0:T(8,128)} %stack.108), calls=%async_computation.2 | async-start | bytes 327680 | tf_op jit(solution)/shard_map/all_to_all | solution.py:24
  54.8 27.5 %all_gather.73 = bf16[16,2,192,64]{2,3,1,0:T(8,128)(2,1)S(1)} all-gather(bf16[1,2,192,64]{2,3,1,0:T(8,128)(2,1)S(1)} %slice_bitcast_fusion.11), channel_id=1, replica_groups=mesh['row'=16,'col'=8] {'row'}, dimensions={0}, use_global_device_ids=true | all-gather | bytes 835584 | tf_op jit(solution)/shard_map/all_gather | solution.py:52
  83.6 1.7 reshape_squeeze.27
  86.8 2.1 fusion.5
  89.1 22.4 %all-gather.6 = f32[16,144,64]{1,2,0:T(8,128)S(1)} all-gather(f32[1,144,64]{1,2,0:T(8,128)S(1)} %get-tuple-element.84), channel_id=2, replica_groups=mesh['row'=16,'col'=8] {'row'}, dimensions={0}, use_global_device_ids=true | all-gather | bytes 626688 | tf_op jit(solution)/shard_map/all_gather | solution.py:52
  111.9 2.7 fusion.96
  115.3 5.6 %all-to-all-start.3 = ((f32[8,1,768]{2,1,0:T(1,128)}), f32[8,1,768]{2,1,0:T(1,128)S(1)}, u32[]{:S(2)}, u32[]{:S(2)}) async-start(f32[8,1,768]{2,1,0:T(1,128)} %reshape.2164), calls=%async_computation.3 | async-start | bytes 49152 | tf_op jit(solution)/shard_map/all_to_all | solution.py:44
  121.1 1.3 fusion.34
  122.4 4.7 all-to-all-done.3
  131.6 2.8 fusion.2
  135.2 1.6 constant_dynamic-slice_fusion.9
  136.9 1.0 copy.452
  137.9 1.8 fusion.28
  140.0 2.1 concatenate.99
  142.1 34.6 %reduce-scatter.4.cloned.1.call-done = f32[2028,8]{0,1:T(8,128)} async-done(((f32[2028,64]{0,1:T(8,128)}), f32[2028,8]{0,1:T(8,128)}) %reduce-scatter.4.cloned.1.call-update) | async-done | bytes 64912 | tf_op jit(solution)/shard_map/reduce_scatter | solution.py:61
  181.2 1.8 fusion.97
  187.9 3.4 all-to-all-start.4
  191.6 6.0 %all-to-all-done.4 = bf16[8,3,192,8]{2,3,1,0:T(8,128)(2,1)S(1)} async-done(((bf16[8,3,192,8]{2,3,1,0:T(8,128)(2,1)}), bf16[8,3,192,8]{2,3,1,0:T(8,128)(2,1)S(1)}, u32[]{:S(2)}, u32[]{:S(2)}) %all-to-all-start.4) | async-done | bytes 73760 | tf_op jit(solution)/shard_map/all_to_all | solution.py:44
  198.3 3.4 all-to-all-start.5
  201.8 27.0 %all_gather.79 = bf16[16,2,192,64]{2,3,1,0:T(8,128)(2,1)S(1)} all-gather(bf16[1,2,192,64]{2,3,1,0:T(8,128)(2,1)S(1)} %slice_bitcast_fusion.8), channel_id=1, replica_groups=mesh['row'=16,'col'=8] {'row'}, dimensions={0}, use_global_device_ids=true | all-gather | bytes 835584 | tf_op jit(solution)/shard_map/all_gather | solution.py:52
  230.2 1.7 reshape_squeeze.30
  233.3 2.1 fusion.8
  235.6 22.4 %all-gather.8 = f32[16,144,64]{1,2,0:T(8,128)S(1)} all-gather(f32[1,144,64]{1,2,0:T(8,128)S(1)} %get-tuple-element.82), channel_id=4, replica_groups=mesh['row'=16,'col'=8] {'row'}, dimensions={0}, use_global_device_ids=true | all-gather | bytes 626688 | tf_op jit(solution)/shard_map/all_gather | solution.py:52
  258.4 2.7 fusion.99
  261.8 5.5 %all-to-all-start.6 = ((f32[8,1,768]{2,1,0:T(1,128)}), f32[8,1,768]{2,1,0:T(1,128)S(1)}, u32[]{:S(2)}, u32[]{:S(2)}) async-start(f32[8,1,768]{2,1,0:T(1,128)} %reshape.2166), calls=%async_computation.7 | async-start | bytes 49152 | tf_op jit(solution)/shard_map/all_to_all | solution.py:44
  267.6 1.9 fusion.36
  269.5 4.0 all-to-all-done.6
  273.5 1.3 reduce.1
  277.8 1.0 convolution_multiply_fusion.7
  279.5 2.8 fusion.3
  283.2 1.6 constant_dynamic-slice_fusion.5
  284.9 1.0 copy.456
  285.9 1.9 fusion.27
  287.9 2.1 concatenate.109
  290.0 34.5 %reduce-scatter.6.cloned.1.call-done = f32[2028,8]{0,1:T(8,128)} async-done(((f32[2028,64]{0,1:T(8,128)}), f32[2028,8]{0,1:T(8,128)}) %reduce-scatter.6.cloned.1.call-update) | async-done | bytes 64912 | tf_op jit(solution)/shard_map/reduce_scatter | solution.py:61
  329.6 2.6 fusion.100
  337.2 3.4 all-to-all-start.7
  340.9 6.0 %all-to-all-done.7 = bf16[8,3,192,8]{2,3,1,0:T(8,128)(2,1)S(1)} async-done(((bf16[8,3,192,8]{2,3,1,0:T(8,128)(2,1)}), bf16[8,3,192,8]{2,3,1,0:T(8,128)(2,1)S(1)}, u32[]{:S(2)}, u32[]{:S(2)}) %all-to-all-start.7) | async-done | bytes 73760 | tf_op jit(solution)/shard_map/all_to_all | solution.py:44
  347.7 3.4 all-to-all-start.8
  351.1 27.0 %all_gather.85 = bf16[16,2,192,64]{2,3,1,0:T(8,128)(2,1)S(1)} all-gather(bf16[1,2,192,64]{2,3,1,0:T(8,128)(2,1)S(1)} %slice_bitcast_fusion.5), channel_id=1, replica_groups=mesh['row'=16,'col'=8] {'row'}, dimensions={0}, use_global_device_ids=true | all-gather | bytes 835584 | tf_op jit(solution)/shard_map/all_gather | solution.py:52
  379.5 1.7 reshape_squeeze.33
  382.6 2.1 fusion.11
  384.9 22.4 %all-gather.10 = f32[16,144,64]{1,2,0:T(8,128)S(1)} all-gather(f32[1,144,64]{1,2,0:T(8,128)S(1)} %get-tuple-element.80), channel_id=6, replica_groups=mesh['row'=16,'col'=8] {'row'}, dimensions={0}, use_global_device_ids=true | all-gather | bytes 626688 | tf_op jit(solution)/shard_map/all_gather | solution.py:52
  407.6 2.7 fusion.102
  411.0 5.2 %all-to-all-start.9 = ((f32[8,1,768]{2,1,0:T(1,128)}), f32[8,1,768]{2,1,0:T(1,128)S(1)}, u32[]{:S(2)}, u32[]{:S(2)}) async-start(f32[8,1,768]{2,1,0:T(1,128)} %reshape.2168), calls=%async_computation.11 | async-start | bytes 49152 | tf_op jit(solution)/shard_map/all_to_all | solution.py:44
  416.6 1.9 fusion.38
  418.5 4.0 all-to-all-done.9
  422.5 1.3 reduce.2
  428.4 2.8 fusion.4
  432.1 1.6 constant_dynamic-slice_fusion.1
  433.8 1.0 copy.460
  434.8 1.9 fusion.26
  436.8 2.1 concatenate.119
  438.9 35.0 %reduce-scatter.8.cloned.1.call-done = f32[2028,8]{0,1:T(8,128)} async-done(((f32[2028,64]{0,1:T(8,128)}), f32[2028,8]{0,1:T(8,128)}) %reduce-scatter.8.cloned.1.call-update) | async-done | bytes 64912 | tf_op jit(solution)/shard_map/reduce_scatter | solution.py:61
  478.8 2.5 fusion.103
  (490 shorter events, 68.7 us)
Async XLA Ops:
  7.2 173.9 %copy-start = (f32[2112,384]{1,0:T(8,128)S(1)}, f32[2112,384]{1,0:T(8,128)}, u32[]{:S(2)}) copy-start(f32[2112,384]{1,0:T(8,128)} %param.28) | copy-start | bytes 9732100
  8.7 24.9 %all-to-all-start = ((s32[128,8,2]{1,2,0:T(2,128)}), s32[128,8,2]{1,2,0:T(2,128)S(1)}, u32[]{:S(2)}, u32[]{:S(2)}) async-start(s32[128,8,2]{1,2,0:T(2,128)} %stack.94), calls=%async_computation | async-start | bytes 262144 | tf_op jit(solution)/shard_map/all_to_all | solution.py:24
  34.2 13.2 %all-to-all-start.1 = ((bf16[8,3,192,8]{2,3,1,0:T(8,128)(2,1)}), bf16[8,3,192,8]{2,3,1,0:T(8,128)(2,1)}, u32[]{:S(2)}, u32[]{:S(2)}) async-start(bf16[8,3,192,8]{2,3,1,0:T(8,128)(2,1)} %broadcast_in_dim.51), calls=%async_computation.1 | async-start | bytes 196608 | tf_op jit(solution)/shard_map/all_to_all | solution.py:44
  47.4 64.4 %copy-start.89 = (pred[64,128]{1,0:T(8,128)(4,1)}, pred[64,128]{1,0:T(8,128)(4,1)S(1)}, u32[]{:S(2)}) copy-start(pred[64,128]{1,0:T(8,128)(4,1)S(1)} %broadcast_and_fusion) | copy-start | bytes 24580
  48.1 37.9 %all-to-all-start.2 = ((f32[8,8,576]{2,1,0:T(8,128)}), f32[8,8,576]{2,1,0:T(8,128)S(1)}, u32[]{:S(2)}, u32[]{:S(2)}) async-start(f32[8,8,576]{2,1,0:T(8,128)} %stack.108), calls=%async_computation.2 | async-start | bytes 327680 | tf_op jit(solution)/shard_map/all_to_all | solution.py:24
  53.8 81.4 %all-gather.16.cloned.1.call-start = ((), (), s32[]{:S(2)}) async-start(), calls=%async_computation.16 | async-start | bytes 1671168 | tf_op jit(solution)/shard_map/all_gather | solution.py:52
  115.3 11.8 %all-to-all-start.3 = ((f32[8,1,768]{2,1,0:T(1,128)}), f32[8,1,768]{2,1,0:T(1,128)S(1)}, u32[]{:S(2)}, u32[]{:S(2)}) async-start(f32[8,1,768]{2,1,0:T(1,128)} %reshape.2164), calls=%async_computation.3 | async-start | bytes 49152 | tf_op jit(solution)/shard_map/all_to_all | solution.py:44
  120.8 55.9 %reduce-scatter.4.cloned.1.call-start = ((), (), s32[]{:S(2)}) async-start(), calls=%async_computation.13 | async-start | bytes 589824 | tf_op jit(solution)/shard_map/reduce_scatter | solution.py:61
  139.8 39.2 %copy-start.66 = (f32[8]{0:T(128)S(1)}, f32[8]{0:T(128)}, u32[]{:S(2)}) copy-start(f32[8]{0:T(128)} %copy-done.65) | copy-start | bytes 100
  139.8 39.2 %copy-start.68 = (f32[8]{0:T(128)S(1)}, f32[8]{0:T(128)}, u32[]{:S(2)}) copy-start(f32[8]{0:T(128)} %copy-done.67) | copy-start | bytes 100
  139.8 39.2 %copy-start.70 = (f32[8]{0:T(128)S(1)}, f32[8]{0:T(128)}, u32[]{:S(2)}) copy-start(f32[8]{0:T(128)} %copy-done.69) | copy-start | bytes 100
  139.8 39.2 %copy-start.72 = (f32[8]{0:T(128)S(1)}, f32[8]{0:T(128)}, u32[]{:S(2)}) copy-start(f32[8]{0:T(128)} %copy-done.71) | copy-start | bytes 100
  139.8 39.2 %copy-start.74 = (f32[8]{0:T(128)S(1)}, f32[8]{0:T(128)}, u32[]{:S(2)}) copy-start(f32[8]{0:T(128)} %copy-done.73) | copy-start | bytes 100
  139.8 39.2 %copy-start.76 = (f32[8]{0:T(128)S(1)}, f32[8]{0:T(128)}, u32[]{:S(2)}) copy-start(f32[8]{0:T(128)} %copy-done.75) | copy-start | bytes 100
  139.8 39.2 %copy-start.78 = (f32[8]{0:T(128)S(1)}, f32[8]{0:T(128)}, u32[]{:S(2)}) copy-start(f32[8]{0:T(128)} %copy-done.77) | copy-start | bytes 100
  139.8 39.2 %copy-start.80 = (f32[8]{0:T(128)S(1)}, f32[8]{0:T(128)}, u32[]{:S(2)}) copy-start(f32[8]{0:T(128)} %copy-done.79) | copy-start | bytes 100
  139.8 39.2 %copy-start.82 = (f32[8]{0:T(128)S(1)}, f32[8]{0:T(128)}, u32[]{:S(2)}) copy-start(f32[8]{0:T(128)} %copy-done.81) | copy-start | bytes 100
  139.9 39.2 %copy-start.84 = (f32[8]{0:T(128)S(1)}, f32[8]{0:T(128)}, u32[]{:S(2)}) copy-start(f32[8]{0:T(128)} %copy-done.83) | copy-start | bytes 100
  139.9 39.2 %copy-start.86 = (f32[8]{0:T(128)S(1)}, f32[8]{0:T(128)}, u32[]{:S(2)}) copy-start(f32[8]{0:T(128)} %copy-done.85) | copy-start | bytes 100
  139.9 39.2 %copy-start.88 = (f32[8]{0:T(128)S(1)}, f32[8]{0:T(128)}, u32[]{:S(2)}) copy-start(f32[8]{0:T(128)} %copy-done.87) | copy-start | bytes 100
  139.9 41.2 %copy-start.16 = (f32[8,384]{1,0:T(8,128)S(1)}, f32[8,384]{1,0:T(8,128)}, u32[]{:S(2)}) copy-start(f32[8,384]{1,0:T(8,128)} %param.20) | copy-start | bytes 36868
  186.4 11.9 %copy-start.54 = (f32[1,8]{1,0:T(1,128)}, f32[1,8]{1,0:T(1,128)S(1)}, u32[]{:S(2)}) copy-start(f32[1,8]{1,0:T(1,128)S(1)} %get-tuple-element.125) | copy-start | bytes 100
  186.5 43.0 %copy-start.22 = (f32[1,8]{1,0:T(1,128)}, f32[1,8]{1,0:T(1,128)S(1)}, u32[]{:S(2)}) copy-start(f32[1,8]{1,0:T(1,128)S(1)} %get-tuple-element.119) | copy-start | bytes 100
  186.5 11.8 %copy-start.44 = (f32[1,8]{1,0:T(1,128)}, f32[1,8]{1,0:T(1,128)S(1)}, u32[]{:S(2)}) copy-start(f32[1,8]{1,0:T(1,128)S(1)} %get-tuple-element.122) | copy-start | bytes 100
  186.5 11.7 %copy-start.46 = (f32[1,8]{1,0:T(1,128)}, f32[1,8]{1,0:T(1,128)S(1)}, u32[]{:S(2)}) copy-start(f32[1,8]{1,0:T(1,128)S(1)} %get-tuple-element.118) | copy-start | bytes 100
  186.6 11.7 %copy-start.48 = (f32[1,8]{1,0:T(1,128)}, f32[1,8]{1,0:T(1,128)S(1)}, u32[]{:S(2)}) copy-start(f32[1,8]{1,0:T(1,128)S(1)} %get-tuple-element.116) | copy-start | bytes 100
  186.6 11.7 %copy-start.50 = (f32[1,8]{1,0:T(1,128)}, f32[1,8]{1,0:T(1,128)S(1)}, u32[]{:S(2)}) copy-start(f32[1,8]{1,0:T(1,128)S(1)} %get-tuple-element.117) | copy-start | bytes 100
  187.9 9.7 %all-to-all-start.4 = ((bf16[8,3,192,8]{2,3,1,0:T(8,128)(2,1)}), bf16[8,3,192,8]{2,3,1,0:T(8,128)(2,1)S(1)}, u32[]{:S(2)}, u32[]{:S(2)}) async-start(bf16[8,3,192,8]{2,3,1,0:T(8,128)(2,1)} %broadcast_in_dim.54), calls=%async_computation.5 | async-start | bytes 196608 | tf_op jit(solution)/shard_map/all_to_all | solution.py:44
  198.3 34.3 %all-to-all-start.5 = ((f32[8,8,576]{2,1,0:T(8,128)}), f32[8,8,576]{2,1,0:T(8,128)S(1)}, u32[]{:S(2)}, u32[]{:S(2)}) async-start(f32[8,8,576]{2,1,0:T(8,128)} %stack.123), calls=%async_computation.6 | async-start | bytes 327680 | tf_op jit(solution)/shard_map/all_to_all | solution.py:24
  201.7 81.5 %all-gather.18.cloned.1.call-start = ((), (), s32[]{:S(2)}) async-start(), calls=%async_computation.17 | async-start | bytes 1671168 | tf_op jit(solution)/shard_map/all_gather | solution.py:52
  261.1 16.7 %copy-start.13 = (f32[12,64]{1,0:T(8,128)}, f32[12,64]{1,0:T(8,128)S(1)}, u32[]{:S(2)}) copy-start(f32[12,64]{1,0:T(8,128)S(1)} %get-tuple-element.229) | copy-start | bytes 9220
  261.8 11.7 %all-to-all-start.6 = ((f32[8,1,768]{2,1,0:T(1,128)}), f32[8,1,768]{2,1,0:T(1,128)S(1)}, u32[]{:S(2)}, u32[]{:S(2)}) async-start(f32[8,1,768]{2,1,0:T(1,128)} %reshape.2166), calls=%async_computation.7 | async-start | bytes 49152 | tf_op jit(solution)/shard_map/all_to_all | solution.py:44
  267.3 57.2 %reduce-scatter.6.cloned.1.call-start = ((), (), s32[]{:S(2)}) async-start(), calls=%async_computation.14 | async-start | bytes 589824 | tf_op jit(solution)/shard_map/reduce_scatter | solution.py:61
  329.5 6.0 %copy-start.21 = (f32[1,8]{1,0:T(1,128)S(1)}, f32[1,8]{1,0:T(1,128)}, u32[]{:S(2)}) copy-start(f32[1,8]{1,0:T(1,128)} %copy-done.20) | copy-start | bytes 100
  329.5 6.0 %copy-start.45 = (f32[1,8]{1,0:T(1,128)S(1)}, f32[1,8]{1,0:T(1,128)}, u32[]{:S(2)}) copy-start(f32[1,8]{1,0:T(1,128)} %copy-done.44) | copy-start | bytes 100
  329.6 6.1 %copy-start.23 = (f32[1,8]{1,0:T(1,128)S(1)}, f32[1,8]{1,0:T(1,128)}, u32[]{:S(2)}) copy-start(f32[1,8]{1,0:T(1,128)} %copy-done.22) | copy-start | bytes 100
  329.6 6.1 %copy-start.49 = (f32[1,8]{1,0:T(1,128)S(1)}, f32[1,8]{1,0:T(1,128)}, u32[]{:S(2)}) copy-start(f32[1,8]{1,0:T(1,128)} %copy-done.48) | copy-start | bytes 100
  329.6 6.1 %copy-start.51 = (f32[1,8]{1,0:T(1,128)S(1)}, f32[1,8]{1,0:T(1,128)}, u32[]{:S(2)}) copy-start(f32[1,8]{1,0:T(1,128)} %copy-done.50) | copy-start | bytes 100
  329.6 6.1 %copy-start.55 = (f32[1,8]{1,0:T(1,128)S(1)}, f32[1,8]{1,0:T(1,128)}, u32[]{:S(2)}) copy-start(f32[1,8]{1,0:T(1,128)} %copy-done.54) | copy-start | bytes 100
  335.7 11.9 %copy-start.60 = (f32[1,8]{1,0:T(1,128)}, f32[1,8]{1,0:T(1,128)S(1)}, u32[]{:S(2)}) copy-start(f32[1,8]{1,0:T(1,128)S(1)} %get-tuple-element.184) | copy-start | bytes 100
  335.8 11.8 %copy-start.32 = (f32[1,8]{1,0:T(1,128)}, f32[1,8]{1,0:T(1,128)S(1)}, u32[]{:S(2)}) copy-start(f32[1,8]{1,0:T(1,128)S(1)} %get-tuple-element.157) | copy-start | bytes 100
  335.8 11.8 %copy-start.34 = (f32[1,8]{1,0:T(1,128)}, f32[1,8]{1,0:T(1,128)S(1)}, u32[]{:S(2)}) copy-start(f32[1,8]{1,0:T(1,128)S(1)} %get-tuple-element.158) | copy-start | bytes 100
  335.8 11.8 %copy-start.36 = (f32[1,8]{1,0:T(1,128)}, f32[1,8]{1,0:T(1,128)S(1)}, u32[]{:S(2)}) copy-start(f32[1,8]{1,0:T(1,128)S(1)} %get-tuple-element.159) | copy-start | bytes 100
  335.8 11.8 %copy-start.24 = (f32[1,8]{1,0:T(1,128)}, f32[1,8]{1,0:T(1,128)S(1)}, u32[]{:S(2)}) copy-start(f32[1,8]{1,0:T(1,128)S(1)} %get-tuple-element.152) | copy-start | bytes 100
  335.9 11.8 %copy-start.26 = (f32[1,8]{1,0:T(1,128)}, f32[1,8]{1,0:T(1,128)S(1)}, u32[]{:S(2)}) copy-start(f32[1,8]{1,0:T(1,128)S(1)} %get-tuple-element.153) | copy-start | bytes 100
  335.9 11.7 %copy-start.38 = (f32[1,8]{1,0:T(1,128)}, f32[1,8]{1,0:T(1,128)S(1)}, u32[]{:S(2)}) copy-start(f32[1,8]{1,0:T(1,128)S(1)} %get-tuple-element.154) | copy-start | bytes 100
  335.9 11.7 %copy-start.40 = (f32[1,8]{1,0:T(1,128)}, f32[1,8]{1,0:T(1,128)S(1)}, u32[]{:S(2)}) copy-start(f32[1,8]{1,0:T(1,128)S(1)} %get-tuple-element.155) | copy-start | bytes 100
  335.9 11.7 %copy-start.42 = (f32[1,8]{1,0:T(1,128)}, f32[1,8]{1,0:T(1,128)S(1)}, u32[]{:S(2)}) copy-start(f32[1,8]{1,0:T(1,128)S(1)} %get-tuple-element.156) | copy-start | bytes 100
  337.2 9.7 %all-to-all-start.7 = ((bf16[8,3,192,8]{2,3,1,0:T(8,128)(2,1)}), bf16[8,3,192,8]{2,3,1,0:T(8,128)(2,1)S(1)}, u32[]{:S(2)}, u32[]{:S(2)}) async-start(bf16[8,3,192,8]{2,3,1,0:T(8,128)(2,1)} %broadcast_in_dim.56), calls=%async_computation.9 | async-start | bytes 196608 | tf_op jit(solution)/shard_map/all_to_all | solution.py:44
  347.7 34.2 %all-to-all-start.8 = ((f32[8,8,576]{2,1,0:T(8,128)}), f32[8,8,576]{2,1,0:T(8,128)S(1)}, u32[]{:S(2)}, u32[]{:S(2)}) async-start(f32[8,8,576]{2,1,0:T(8,128)} %stack.138), calls=%async_computation.10 | async-start | bytes 327680 | tf_op jit(solution)/shard_map/all_to_all | solution.py:24
  351.1 81.1 %all-gather.20.cloned.1.call-start = ((), (), s32[]{:S(2)}) async-start(), calls=%async_computation.18 | async-start | bytes 1671168 | tf_op jit(solution)/shard_map/all_gather | solution.py:52
  410.3 16.4 %copy-start.12 = (f32[12,64]{1,0:T(8,128)}, f32[12,64]{1,0:T(8,128)S(1)}, u32[]{:S(2)}) copy-start(f32[12,64]{1,0:T(8,128)S(1)} %get-tuple-element.235) | copy-start | bytes 9220
  411.0 11.5 %all-to-all-start.9 = ((f32[8,1,768]{2,1,0:T(1,128)}), f32[8,1,768]{2,1,0:T(1,128)S(1)}, u32[]{:S(2)}, u32[]{:S(2)}) async-start(f32[8,1,768]{2,1,0:T(1,128)} %reshape.2168), calls=%async_computation.11 | async-start | bytes 49152 | tf_op jit(solution)/shard_map/all_to_all | solution.py:44
  416.3 57.6 %reduce-scatter.8.cloned.1.call-start = ((), (), s32[]{:S(2)}) async-start(), calls=%async_computation.15 | async-start | bytes 589824 | tf_op jit(solution)/shard_map/reduce_scatter | solution.py:61
  438.9 44.7 %copy-start.39 = (f32[1,8]{1,0:T(1,128)S(1)}, f32[1,8]{1,0:T(1,128)}, u32[]{:S(2)}) copy-start(f32[1,8]{1,0:T(1,128)} %copy-done.38) | copy-start | bytes 100
  438.9 44.7 %copy-start.41 = (f32[1,8]{1,0:T(1,128)S(1)}, f32[1,8]{1,0:T(1,128)}, u32[]{:S(2)}) copy-start(f32[1,8]{1,0:T(1,128)} %copy-done.40) | copy-start | bytes 100
  438.9 44.7 %copy-start.43 = (f32[1,8]{1,0:T(1,128)S(1)}, f32[1,8]{1,0:T(1,128)}, u32[]{:S(2)}) copy-start(f32[1,8]{1,0:T(1,128)} %copy-done.42) | copy-start | bytes 100
  474.6 9.8 %copy-start.25 = (f32[1,8]{1,0:T(1,128)S(1)}, f32[1,8]{1,0:T(1,128)}, u32[]{:S(2)}) copy-start(f32[1,8]{1,0:T(1,128)} %copy-done.24) | copy-start | bytes 100
  474.6 9.8 %copy-start.27 = (f32[1,8]{1,0:T(1,128)S(1)}, f32[1,8]{1,0:T(1,128)}, u32[]{:S(2)}) copy-start(f32[1,8]{1,0:T(1,128)} %copy-done.26) | copy-start | bytes 100
  474.6 9.8 %copy-start.61 = (f32[1,8]{1,0:T(1,128)S(1)}, f32[1,8]{1,0:T(1,128)}, u32[]{:S(2)}) copy-start(f32[1,8]{1,0:T(1,128)} %copy-done.60) | copy-start | bytes 100
  474.7 9.7 %copy-start.33 = (f32[1,8]{1,0:T(1,128)S(1)}, f32[1,8]{1,0:T(1,128)}, u32[]{:S(2)}) copy-start(f32[1,8]{1,0:T(1,128)} %copy-done.32) | copy-start | bytes 100
  474.7 9.7 %copy-start.35 = (f32[1,8]{1,0:T(1,128)S(1)}, f32[1,8]{1,0:T(1,128)}, u32[]{:S(2)}) copy-start(f32[1,8]{1,0:T(1,128)} %copy-done.34) | copy-start | bytes 100
  474.7 9.7 %copy-start.37 = (f32[1,8]{1,0:T(1,128)S(1)}, f32[1,8]{1,0:T(1,128)}, u32[]{:S(2)}) copy-start(f32[1,8]{1,0:T(1,128)} %copy-done.36) | copy-start | bytes 100
  474.7 9.8 %copy-start.59 = (f32[1,8]{1,0:T(1,128)S(1)}, f32[1,8]{1,0:T(1,128)}, u32[]{:S(2)}) copy-start(f32[1,8]{1,0:T(1,128)} %copy-done.58) | copy-start | bytes 100
  (49 other events, 119.6 us)
Sparse Core Ops, SparseCore 0:
  86.9 44.2 all-gather.15
  142.3 34.4 reduce-scatter.3
  233.5 44.0 all-gather.17
  290.1 34.3 reduce-scatter.5
  382.7 44.0 all-gather.19
  439.0 34.8 reduce-scatter.7
